TPU v7x, 32 devices: a whole 2x2x4 slice. The times are simulated.
32 devices in a mesh: row: 4 (over z), col: 8 (over y, x, core).
Axes of the slice: x: 2, y: 2, z: 4, core: 2. Of those that a mesh axis runs over, the one named last changes fastest.
Arguments:
- fine_residual: bfloat16 [16, 524288], P(None, ('row', 'col')), may hold values from -6 to 6
- tiles_one: bfloat16 [8192, 128, 128], P(('row', 'col')), may hold values from -0.1875 to 0.1875
- pointers_one: int32 [4128], P(('row', 'col')), may hold values from 0 to 256, as said below
- columns_one: int32 [8192], P(('row', 'col')), may hold values from 0 to 1023, as said below
- points_one: int32 [131072], P(('col', 'row')), may hold values from 0 to 16383, as said below
- tiles_two: bfloat16 [4096, 128, 128], P(('row', 'col')), may hold values from -0.125 to 0.125
- pointers_two: int32 [2080], P(('row', 'col')), may hold values from 0 to 128, as said below
- columns_two: int32 [4096], P(('row', 'col')), may hold values from 0 to 127
- points_two: int32 [32768], P(('row', 'col')), may hold values from 0 to 4095, as said below
- tiles_three: bfloat16 [512, 128, 128], P(('row', 'col')), may hold values from -0.1875 to 0.1875
- pointers_three: int32 [288], P(('row', 'col')), may hold values from 0 to 16, as said below
- columns_three: int32 [512], P(('row', 'col')), may hold values from 0 to 63
- points_three: int32 [8192], P(('col', 'row')), may hold values from 0 to 1023, as said below
Outputs:
- coarse_one: bfloat16 [16, 131072], P(None, ('col', 'row'))
- coarse_two: bfloat16 [16, 32768], P(None, ('row', 'col'))
- coarse_three: bfloat16 [16, 8192], P(None, ('col', 'row'))
Inputs may be any that keep to these rules, and one draw needn't show every extreme that they name: `pointers_one`: each tile set's 128 + 1 pointers start at 0 and never fall; the last is that set's live slot count, at most 256; some set has 256 live slots. `pointers_two`: each tile set's 64 + 1 pointers start at 0 and never fall; the last is that set's live slot count, at most 128; some set has 128 live slots. `pointers_three`: each tile set's 8 + 1 pointers start at 0 and never fall; the last is that set's live slot count, at most 16; some set has 16 live slots. `columns_one`: among the live slots of one tile set, at most 32 name block columns with the same quotient by 128; some set reaches 32. `points_one`: values are distinct within each aligned run of 4096 entries. `points_two`: values are distinct within each aligned run of 1024 entries. `points_three`: values are distinct within each aligned run of 256 entries.
All inputs are finite; a program needn't handle non-finite values.
Results may differ from a plain program's by a relative error of at most 0.0057.
Values may be sent and summed in bfloat16 or wider, within the bound.
No kernel may reach another device: no remote copies, remote signals or barrier semaphores. Data moves between devices by JAX's collectives and lax.ppermute only.
A program may use at most 128 MiB of HBM per device.

v0:
```python
import jax
import jax.numpy as jnp
from jax import lax
from jax.sharding import PartitionSpec as P


def slot_layout(pointers, slot_count):
    block_count = pointers.shape[0] - 1
    positions = jnp.arange(slot_count, dtype=jnp.int32)
    is_live = positions < pointers[block_count]
    finished = jnp.sum((pointers[1:][None, :] <= positions[:, None]).astype(jnp.int32), axis=1)
    segment = jnp.where(is_live, finished, block_count)
    return (is_live, segment)


def block_sums(products, segment, block_count):
    summed = jax.ops.segment_sum(
        products, segment, num_segments=block_count + 1, indices_are_sorted=True
    )
    summed = summed[:block_count]
    return jnp.transpose(summed, (1, 0, 2)).reshape(summed.shape[1], block_count * summed.shape[2])


def group_products(tiles, fine_group, columns, segment, block_count):
    vector_count = fine_group.shape[0]
    tile_edge = tiles.shape[1]
    blocks = fine_group.reshape(vector_count, fine_group.shape[1] // tile_edge, tile_edge)
    picked = jnp.take(blocks, columns, axis=1)
    products = jnp.einsum("sij,vsj->svi", tiles, picked, preferred_element_type=jnp.float32)
    return block_sums(products, segment, block_count)


def add_points(partial_value, own_piece, points, position):
    injected = jnp.take(own_piece, points, axis=1).astype(jnp.float32)
    offset = position * points.shape[0]
    current = lax.dynamic_slice_in_dim(partial_value, offset, points.shape[0], 1)
    return lax.dynamic_update_slice_in_dim(partial_value, current + injected, offset, 1)


def on_device(
    fine_residual,
    tiles_one,
    pointers_one,
    columns_one,
    points_one,
    tiles_two,
    pointers_two,
    columns_two,
    points_two,
    tiles_three,
    pointers_three,
    columns_three,
    points_three,
):
    tile_edge = tiles_one.shape[1]
    vector_count = fine_residual.shape[0]
    slots_first = tiles_one.shape[0]
    blocks_first = pointers_one.shape[0] - 1
    live_first, segment_first = slot_layout(pointers_one, slots_first)
    peer_count = lax.axis_size("col")
    per_peer = slots_first // peer_count
    blocks_peer = fine_residual.shape[1] // tile_edge
    owner_peer = columns_one // blocks_peer
    within = columns_one % blocks_peer
    peer_ids = jnp.arange(peer_count, dtype=jnp.int32)
    peer_hits = ((owner_peer[:, None] == peer_ids[None, :]) & live_first[:, None]).astype(jnp.int32)
    peer_rank = jnp.sum(jnp.cumsum(peer_hits, axis=0) * peer_hits, axis=1) - 1
    target = jnp.where(live_first, owner_peer * per_peer + peer_rank, peer_count * per_peer)
    requests = jnp.zeros((peer_count * per_peer,), jnp.int32).at[target].set(within, mode="drop")
    requests = requests.reshape(peer_count, per_peer)
    own_blocks = jnp.transpose(
        fine_residual.reshape(vector_count, blocks_peer, tile_edge), (1, 0, 2)
    )
    found_blocks = jnp.take(
        own_blocks, lax.all_to_all(requests, "col", split_axis=0, concat_axis=0, tiled=True), axis=0
    )
    replies = lax.all_to_all(found_blocks, "col", split_axis=0, concat_axis=0, tiled=True)
    flat_replies = replies.reshape(peer_count * per_peer, vector_count, tile_edge)
    picked = jnp.take(flat_replies, jnp.minimum(target, peer_count * per_peer - 1), axis=0)
    products = jnp.einsum("sij,svj->svi", tiles_one, picked, preferred_element_type=jnp.float32)
    partial_one = block_sums(products, segment_first, blocks_first)
    partial_one = add_points(partial_one, fine_residual, points_one, lax.axis_index("row"))
    coarse_one = lax.psum_scatter(partial_one, "row", scatter_dimension=1, tiled=True).astype(
        jnp.bfloat16
    )
    group_one = lax.all_gather(coarse_one, "row", axis=1, tiled=True)
    segment_second = slot_layout(pointers_two, tiles_two.shape[0])[1]
    partial_two = group_products(
        tiles_two, group_one, columns_two, segment_second, pointers_two.shape[0] - 1
    )
    partial_two = add_points(partial_two, coarse_one, points_two, lax.axis_index("col"))
    coarse_two = lax.psum_scatter(partial_two, "col", scatter_dimension=1, tiled=True).astype(
        jnp.bfloat16
    )
    group_two = lax.all_gather(coarse_two, "col", axis=1, tiled=True)
    segment_third = slot_layout(pointers_three, tiles_three.shape[0])[1]
    partial_three = group_products(
        tiles_three, group_two, columns_three, segment_third, pointers_three.shape[0] - 1
    )
    partial_three = add_points(partial_three, coarse_two, points_three, lax.axis_index("row"))
    coarse_three = lax.psum_scatter(partial_three, "row", scatter_dimension=1, tiled=True).astype(
        jnp.bfloat16
    )
    return (coarse_one, coarse_two, coarse_three)


def solution(mesh):
    placed = (
        P(None, ("row", "col")),
        P(("row", "col"), None, None),
        P(("row", "col")),
        P(("row", "col")),
        P(("col", "row")),
        P(("row", "col"), None, None),
        P(("row", "col")),
        P(("row", "col")),
        P(("row", "col")),
        P(("row", "col"), None, None),
        P(("row", "col")),
        P(("row", "col")),
        P(("col", "row")),
    )
    return jax.shard_map(
        on_device,
        mesh=mesh,
        in_specs=placed,
        out_specs=(P(None, ("col", "row")), P(None, ("row", "col")), P(None, ("col", "row"))),
        check_vma=False,
    )
```

profile of v0, /device:TPU:0, one launch (start us, length us, event | category | flops | bytes accessed | tf_op | source)
XLA Modules:
  0.0 434.2 jit_solution(3455119433022537755)
XLA Ops:
  7.2 1.3 slice.33
  8.5 0.7 add_compare_fusion
  9.2 0.7 iota_compare_fusion.5
  9.8 0.7 and_select_fusion
  10.5 0.6 reduce-window.6
  11.1 0.2 slice_reduce_fusion
  11.4 0.1 fusion.17
  11.4 0.7 compare_select_fusion.5
  12.1 1.4 scatter_custom_fusion
  13.5 0.7 all_to_all.13
  14.2 5.2 %all-to-all-start = ((s32[8,1,32]{2,1,0:T(1,128)}), s32[8,1,32]{2,1,0:T(1,128)S(1)}, u32[]{:S(2)}, u32[]{:S(2)}) async-start(s32[8,1,32]{2,1,0:T(1,128)} %all_to_all.13), calls=%async_computation | async-start | bytes 8192 | tf_op jit(solution)/shard_map/all_to_all | solution.py:75
  19.4 1.1 bitcast_bitcast_fusion
  20.5 3.5 all-to-all-done
  24.0 0.1 reshape.174
  24.1 0.8 gather_fusion
  25.0 1.3 broadcast_select_fusion
  26.2 3.6 all-to-all-start.1
  29.9 0.1 slice.34
  29.9 3.1 copy.76
  33.0 16.9 %gather_fusion.2 = bf16[4096,16]{1,0:T(8,128)(2,1)} fusion(bf16[16,16384]{0,1:T(8,128)(2,1)} %copy.76, s32[4096]{0:T(1024)S(1)} %fusion.16), kind=kCustom, calls=%fused_computation.2 | custom fusion | bytes 278528 | tf_op jit(solution)/shard_map/jit(_take)/gather | solution.py:34
  50.0 0.7 compare_and_fusion.6
  50.6 0.1 convert_reduce_fusion
  50.8 0.7 compare_select_fusion.7
  51.4 0.8 gather_fusion.1
  52.3 9.3 %fusion.1 = f32[256,16,128]{2,1,0:T(8,128)} fusion(bf16[256,128,128]{2,1,0:T(8,128)(2,1)} %param.14, bf16[256,16,128]{2,1,0:T(8,128)(2,1)S(1)} %gather_fusion.1, pred[256]{0:T(512)(128)(4,1)S(1)} %get-tuple-element.21), kind=kOutput, calls=%fused_computation.14 | convolution fusion | flops 134742016 | bytes 11534592 | tf_op jit(solution)/shard_map/sij,svj->svi/dot_general | solution.py:80
  61.5 0.1 broadcast_in_dim.121
  61.6 20.6 %scatter_fusion = f32[129,16,128]{2,1,0:T(8,128)S(1)} fusion(f32[129,16,128]{2,1,0:T(8,128)S(1)} %broadcast_in_dim.121, s32[256]{0:T(256)S(1)} %bitcast.75, f32[256,16,128]{2,1,0:T(8,128)} %fusion.1), kind=kCustom, calls=%fused_computation.8 | custom fusion | flops 524288 | bytes 6292480 | tf_op jit(solution)/shard_map/scatter-add | solution.py:17
  82.3 0.1 slice_bitcast_fusion
  82.3 4.6 %copy.94 = f32[16,128,128]{0,2,1:T(8,128)} copy(f32[16,128,128]{2,0,1:T(8,128)S(1)} %slice_bitcast_fusion) | data formatting | bytes 2097152 | tf_op jit(solution)/shard_map/reshape | solution.py:21
  87.0 3.0 fusion
  90.0 0.6 copy-done.8
  90.6 0.1 slice.39
  90.7 0.6 slice.38
  91.3 0.1 convert_reduce_fusion.1
  91.4 0.7 fusion.22
  92.1 144.5 %reduce-scatter.4.cloned.1.call-done = f32[16,4096]{0,1:T(8,128)} async-done(((f32[16,16384]{0,1:T(8,128)}), f32[16,4096]{0,1:T(8,128)}) %reduce-scatter.4.cloned.1.call-update) | async-done | bytes 262160 | tf_op jit(solution)/shard_map/reduce_scatter | solution.py:83
  236.6 1.7 convert_element_type.35
  238.3 72.1 %all_gather.6 = bf16[16,16384]{0,1:T(8,128)(2,1)} all-gather(bf16[16,4096]{0,1:T(8,128)(2,1)S(1)} %convert_element_type.35), channel_id=1, replica_groups=mesh['row'=4,'col'=8] {'row'}, dimensions={1}, use_global_device_ids=true | all-gather | bytes 655360 | tf_op jit(solution)/shard_map/all_gather | solution.py:86
  310.4 3.5 copy.79
  313.9 0.7 gather_fusion.3
  314.6 4.5 %fusion.5 = f32[128,16,128]{2,1,0:T(8,128)S(1)} fusion(bf16[128,128,128]{2,1,0:T(8,128)(2,1)} %param.18, bf16[128,16,128]{2,1,0:T(8,128)(2,1)S(1)} %gather_fusion.3, pred[128]{0:T(512)(128)(4,1)S(1)} %compare_and_fusion.5), kind=kOutput, calls=%fused_computation.22 | convolution fusion | flops 67371008 | bytes 5767296 | tf_op jit(solution)/shard_map/sij,vsj->svi/dot_general | solution.py:29
  319.2 5.5 %scatter_fusion.1 = f32[65,16,128]{2,1,0:T(8,128)S(1)} fusion(f32[65,16,128]{2,1,0:T(8,128)S(1)} %broadcast_in_dim.133, s32[128]{0:T(128)S(1)} %fusion.22, f32[128,16,128]{2,1,0:T(8,128)S(1)} %fusion.5), kind=kCustom, calls=%fused_computation.9 | custom fusion | flops 262144 | bytes 3146240 | tf_op jit(solution)/shard_map/scatter-add | solution.py:17
  324.8 2.6 copy.96
  327.3 3.2 gather_fusion.4
  330.6 2.0 fusion.4
  332.7 0.1 slice.42
  332.8 0.6 slice.41
  333.3 0.1 convert_reduce_fusion.2
  333.4 0.6 fusion.23
  334.1 50.5 %reduce-scatter.6.cloned.1.call-done = f32[16,1024]{0,1:T(8,128)} async-done(((f32[16,8192]{0,1:T(8,128)}), f32[16,1024]{0,1:T(8,128)}) %reduce-scatter.6.cloned.1.call-update) | async-done | bytes 65552 | tf_op jit(solution)/shard_map/reduce_scatter | solution.py:92
  384.6 1.1 convert_element_type.38
  385.7 15.3 %all_gather.7 = bf16[16,8192]{0,1:T(8,128)(2,1)} all-gather(bf16[16,1024]{0,1:T(8,128)(2,1)S(1)} %convert_element_type.38), channel_id=1, replica_groups=mesh['row'=4,'col'=8] {'col'}, dimensions={1}, use_global_device_ids=true | all-gather | bytes 294912 | tf_op jit(solution)/shard_map/all_gather | solution.py:95
  401.0 1.9 copy.84
  402.9 0.6 gather_fusion.5
  403.4 0.4 fusion.11
  403.9 1.2 scatter_fusion.2
  405.1 0.1 copy.98
  405.2 0.9 gather_fusion.6
  406.0 0.1 bitcast_add_fusion.2
  406.2 0.6 copy-done.3
  406.9 1.0 copy.88
  407.8 0.7 copy.89
  408.6 17.8 %reduce-scatter.8.cloned.1.call-done = f32[16,256]{1,0:T(8,128)} async-done(((f32[16,1024]{1,0:T(8,128)}), f32[16,256]{1,0:T(8,128)}) %reduce-scatter.8.cloned.1.call-update) | async-done | bytes 16400 | tf_op jit(solution)/shard_map/reduce_scatter | solution.py:101
  426.4 1.3 convert_element_type.41
  (56 shorter events, 0.6 us)
Async XLA Ops:
  7.2 396.3 %copy-start = (bf16[16,128,128]{2,1,0:T(8,128)(2,1)S(1)}, bf16[16,128,128]{2,1,0:T(8,128)(2,1)}, u32[]{:S(2)}) copy-start(bf16[16,128,128]{2,1,0:T(8,128)(2,1)} %param.22) | copy-start | bytes 1572868
  7.2 22.7 %copy-start.7 = (s32[129]{0:T(256)S(1)}, s32[129]{0:T(256)}, u32[]{:S(2)}) copy-start(s32[129]{0:T(256)} %param.15) | copy-start | bytes 1552
  7.2 22.8 %copy-start.1 = (bf16[16,16384]{1,0:T(8,128)(2,1)S(1)}, bf16[16,16384]{1,0:T(8,128)(2,1)}, u32[]{:S(2)}) copy-start(bf16[16,16384]{1,0:T(8,128)(2,1)} %param.13) | copy-start | bytes 1572868
  7.2 22.6 %copy-start.4 = (s32[4096]{0:T(1024)S(1)}, s32[4096]{0:T(1024)}, u32[]{:S(2)}) copy-start(s32[4096]{0:T(1024)} %param.17) | copy-start | bytes 49156
  14.2 9.8 %all-to-all-start = ((s32[8,1,32]{2,1,0:T(1,128)}), s32[8,1,32]{2,1,0:T(1,128)S(1)}, u32[]{:S(2)}, u32[]{:S(2)}) async-start(s32[8,1,32]{2,1,0:T(1,128)} %all_to_all.13), calls=%async_computation | async-start | bytes 8192 | tf_op jit(solution)/shard_map/all_to_all | solution.py:75
  26.2 25.2 %all-to-all-start.1 = ((bf16[8,32,16,128]{3,2,1,0:T(8,128)(2,1)}), bf16[8,32,16,128]{3,2,1,0:T(8,128)(2,1)S(1)}, u32[]{:S(2)}, u32[]{:S(2)}) async-start(bf16[8,32,16,128]{3,2,1,0:T(8,128)(2,1)} %broadcast_select_fusion), calls=%async_computation.1 | async-start | bytes 2097152 | tf_op jit(solution)/shard_map/all_to_all | solution.py:77
  29.8 206.8 %reduce-scatter.4.cloned.1.call-start = ((), (), s32[]{:S(2)}) async-start(), calls=%async_computation.5 | async-start | bytes 10485760 | tf_op jit(solution)/shard_map/reduce_scatter | solution.py:83
  82.3 4.6 %copy-start.2 = (bf16[4096,16]{1,0:T(8,128)(2,1)S(1)}, bf16[4096,16]{1,0:T(8,128)(2,1)}, u32[]{:S(2)}) copy-start(bf16[4096,16]{1,0:T(8,128)(2,1)} %gather_fusion.2) | copy-start | bytes 393220
  89.9 0.7 copy-start.8
  89.9 1.3 copy-start.9
  89.9 1.3 copy-start.11
  89.9 2.1 copy-start.6
  89.9 2.1 copy-start.5
  90.0 294.7 %reduce-scatter.6.cloned.1.call-start = ((), (), s32[]{:S(2)}) async-start(), calls=%async_computation.6 | async-start | bytes 4718592 | tf_op jit(solution)/shard_map/reduce_scatter | solution.py:92
  324.7 7.9 %copy-start.10 = (s32[9]{0:T(128)S(1)}, s32[9]{0:T(128)}, u32[]{:S(2)}) copy-start(s32[9]{0:T(128)} %param.23) | copy-start | bytes 112
  332.6 93.8 %reduce-scatter.8.cloned.1.call-start = ((), (), s32[]{:S(2)}) async-start(), calls=%async_computation.7 | async-start | bytes 81920 | tf_op jit(solution)/shard_map/reduce_scatter | solution.py:101
  406.2 0.6 copy-start.3
Sparse Core Ops, SparseCore 0:
  90.1 146.4 reduce-scatter.3
  332.7 51.8 reduce-scatter.5
  407.0 19.3 reduce-scatter.7
where the time goes:
time: 435 us; the launch traced here: 434 us
  waiting for transfers between devices  216 us (50%)
  blocking collectives  87.4 us (20%)
  local copies, waits for them, and re-layouts  49.2 us (11%)
  other arithmetic  44.1 us (10%)
  matrix products  14.2 us (3%)
  between operations  14.2 us (3%)
  starting transfers between devices  8.88 us (2%)
    reduce_scatter x1, waiting for transfers between devices, on_device(): lax.psum_scatter(partial_one, 'row', scatter_dimension=1, tiled=True)  144 us
    all_gather x1, blocking collectives, on_device(): group_one = lax.all_gather(coarse_one, 'row', axis=1, tiled=True)  72.1 us
    reduce_scatter x1, waiting for transfers between devices, on_device(): lax.psum_scatter(partial_two, 'col', scatter_dimension=1, tiled=True)  50.5 us
    scatter-add x3, other arithmetic, block_sums(): jax.ops.segment_sum(products, segment, num_segments=block_count + 1, indi...  27.3 us
    gather x3, local copies, waits for them, and re-layouts, add_points(): injected = jnp.take(own_piece, points, axis=1).astype(jnp.float32)  21 us
    reduce_scatter x1, waiting for transfers between devices, on_device(): lax.psum_scatter(partial_three, 'row', scatter_dimension=1, tiled=True)  17.8 us
    all_gather x1, blocking collectives, on_device(): group_two = lax.all_gather(coarse_two, 'col', axis=1, tiled=True)  15.3 us
    dot_general x1, matrix products, on_device(): jnp.einsum('sij,svj->svi', tiles_one, picked, preferred_element_type=jnp....  9.25 us
  transfers between devices with their start and end apart: 5, of which 4 were waited for; matrix products, arithmetic and copies ran while one was open for 6% of the time, Pallas kernels for 0%

commit v1 on v0

--- a/solution.py
+++ b/solution.py
@@ -83,7 +83,8 @@
     coarse_one = lax.psum_scatter(partial_one, "row", scatter_dimension=1, tiled=True).astype(
         jnp.bfloat16
     )
-    group_one = lax.all_gather(coarse_one, "row", axis=1, tiled=True)
+    left_arr = lax.all_gather(coarse_one, "row")
+    group_one = jnp.concatenate(left_arr, axis=1)
     segment_second = slot_layout(pointers_two, tiles_two.shape[0])[1]
     partial_two = group_products(
         tiles_two, group_one, columns_two, segment_second, pointers_two.shape[0] - 1

time: 435 us -> 375 us (0.86)
  blocking collectives: 87.4 us -> 30.2 us
    all_gather x1, blocking collectives: 72.1 us -> 16.1 us  [on_device(): left_arr = lax.all_gather(coarse_one, 'row')]
    reshape x2 -> x1, local copies, waits for them, and re-layouts: 5.37 us -> 0.79 us  [group_products(): fine_group.reshape(vector_count, fine_group.shape[1] // tile_edge, tile_e...]
  transfers between devices with their start and end apart: 5 -> 5, of which waited for: 4 -> 4; matrix products, arithmetic and copies ran while one was open for 6% -> 7% of each run, Pallas kernels for 0% -> 0%
where the time goes in v1:
time: 375 us; the launch traced here: 374 us
  waiting for transfers between devices  217 us (58%)
  local copies, waits for them, and re-layouts  45.2 us (12%)
  other arithmetic  44.1 us (12%)
  blocking collectives  30.2 us (8%)
  matrix products  14.2 us (4%)
  between operations  14.2 us (4%)
  starting transfers between devices  8.88 us (2%)
    reduce_scatter x1, waiting for transfers between devices, on_device(): lax.psum_scatter(partial_one, 'row', scatter_dimension=1, tiled=True)  144 us
    reduce_scatter x1, waiting for transfers between devices, on_device(): lax.psum_scatter(partial_two, 'col', scatter_dimension=1, tiled=True)  50 us
    scatter-add x3, other arithmetic, block_sums(): jax.ops.segment_sum(products, segment, num_segments=block_count + 1, indi...  27.3 us
    gather x3, local copies, waits for them, and re-layouts, add_points(): injected = jnp.take(own_piece, points, axis=1).astype(jnp.float32)  21 us
    reduce_scatter x1, waiting for transfers between devices, on_device(): lax.psum_scatter(partial_three, 'row', scatter_dimension=1, tiled=True)  18.9 us
    all_gather x1, blocking collectives, on_device(): left_arr = lax.all_gather(coarse_one, 'row')  16.1 us
    all_gather x1, blocking collectives, on_device(): group_two = lax.all_gather(coarse_two, 'col', axis=1, tiled=True)  14.1 us
    dot_general x1, matrix products, on_device(): jnp.einsum('sij,svj->svi', tiles_one, picked, preferred_element_type=jnp....  9.25 us
  transfers between devices with their start and end apart: 5, of which 4 were waited for; matrix products, arithmetic and copies ran while one was open for 7% of the time, Pallas kernels for 0%

profile of v1, /device:TPU:0, one launch (start us, length us, event | category | flops | bytes accessed | tf_op | source)
XLA Modules:
  0.0 373.7 jit_solution(717970555386842993)
XLA Ops:
  7.2 1.3 slice.33
  8.5 0.7 add_compare_fusion
  9.2 0.7 iota_compare_fusion.5
  9.8 0.7 and_select_fusion
  10.5 0.6 reduce-window.6
  11.1 0.2 slice_reduce_fusion
  11.4 0.1 fusion.17
  11.4 0.7 compare_select_fusion.5
  12.1 1.4 scatter_custom_fusion
  13.5 0.7 all_to_all.13
  14.2 5.2 %all-to-all-start = ((s32[8,1,32]{2,1,0:T(1,128)}), s32[8,1,32]{2,1,0:T(1,128)S(1)}, u32[]{:S(2)}, u32[]{:S(2)}) async-start(s32[8,1,32]{2,1,0:T(1,128)} %all_to_all.13), calls=%async_computation | async-start | bytes 8192 | tf_op jit(solution)/shard_map/all_to_all | solution.py:75
  19.4 1.1 bitcast_bitcast_fusion
  20.5 3.5 all-to-all-done
  24.0 0.1 reshape.174
  24.1 0.8 gather_fusion
  25.0 1.3 broadcast_select_fusion
  26.2 3.6 all-to-all-start.1
  29.9 0.1 slice.34
  29.9 3.1 copy.83
  33.0 16.9 %gather_fusion.2 = bf16[4096,16]{1,0:T(8,128)(2,1)} fusion(bf16[16,16384]{0,1:T(8,128)(2,1)} %copy.83, s32[4096]{0:T(1024)S(1)} %fusion.16), kind=kCustom, calls=%fused_computation.2 | custom fusion | bytes 278528 | tf_op jit(solution)/shard_map/jit(_take)/gather | solution.py:34
  50.0 0.7 compare_and_fusion.6
  50.6 0.1 convert_reduce_fusion
  50.8 0.7 compare_select_fusion.7
  51.4 0.8 gather_fusion.1
  52.3 9.3 %fusion.1 = f32[256,16,128]{2,1,0:T(8,128)} fusion(bf16[256,128,128]{2,1,0:T(8,128)(2,1)} %param.14, bf16[256,16,128]{2,1,0:T(8,128)(2,1)S(1)} %gather_fusion.1, pred[256]{0:T(512)(128)(4,1)S(1)} %get-tuple-element.21), kind=kOutput, calls=%fused_computation.14 | convolution fusion | flops 134742016 | bytes 11534592 | tf_op jit(solution)/shard_map/sij,svj->svi/dot_general | solution.py:80
  61.6 20.6 %scatter_fusion = f32[129,16,128]{2,1,0:T(8,128)S(1)} fusion(f32[129,16,128]{2,1,0:T(8,128)S(1)} %broadcast_in_dim.121, s32[256]{0:T(256)S(1)} %bitcast.77, f32[256,16,128]{2,1,0:T(8,128)} %fusion.1), kind=kCustom, calls=%fused_computation.8 | custom fusion | flops 524288 | bytes 6292480 | tf_op jit(solution)/shard_map/scatter-add | solution.py:17
  82.3 4.6 %copy.100 = f32[16,128,128]{0,2,1:T(8,128)} copy(f32[16,128,128]{2,0,1:T(8,128)S(1)} %slice_bitcast_fusion) | data formatting | bytes 2097152 | tf_op jit(solution)/shard_map/reshape | solution.py:21
  87.0 3.0 fusion
  90.0 0.6 copy-done.9
  90.6 0.1 slice.39
  90.7 0.6 slice.38
  91.3 0.1 convert_reduce_fusion.1
  91.4 0.7 fusion.22
  92.1 144.5 %reduce-scatter.4.cloned.1.call-done = f32[16,4096]{0,1:T(8,128)} async-done(((f32[16,16384]{0,1:T(8,128)}), f32[16,4096]{0,1:T(8,128)}) %reduce-scatter.4.cloned.1.call-update) | async-done | bytes 262160 | tf_op jit(solution)/shard_map/reduce_scatter | solution.py:83
  236.6 1.7 convert_element_type.35
  238.3 0.3 copy.96
  238.6 16.1 %all-gather = bf16[64,4096]{1,0:T(8,128)(2,1)S(1)} all-gather(bf16[16,4096]{1,0:T(8,128)(2,1)S(1)} %copy.96), channel_id=2, replica_groups=mesh['row'=4,'col'=8] {'row'}, dimensions={0}, use_global_device_ids=true | all-gather | bytes 655360 | tf_op jit(solution)/shard_map/all_gather | solution.py:86
  254.7 0.4 copy.86
  255.1 0.5 reshape_reshape.3
  255.6 0.3 copy.87
  256.0 0.7 gather_fusion.3
  256.7 4.5 %fusion.5 = f32[128,16,128]{2,1,0:T(8,128)S(1)} fusion(bf16[128,128,128]{2,1,0:T(8,128)(2,1)} %param.18, bf16[128,16,128]{2,1,0:T(8,128)(2,1)S(1)} %gather_fusion.3, pred[128]{0:T(512)(128)(4,1)S(1)} %compare_and_fusion.5), kind=kOutput, calls=%fused_computation.22 | convolution fusion | flops 67371008 | bytes 5767296 | tf_op jit(solution)/shard_map/sij,vsj->svi/dot_general | solution.py:29
  261.3 5.5 %scatter_fusion.1 = f32[65,16,128]{2,1,0:T(8,128)S(1)} fusion(f32[65,16,128]{2,1,0:T(8,128)S(1)} %broadcast_in_dim.133, s32[128]{0:T(128)S(1)} %fusion.22, f32[128,16,128]{2,1,0:T(8,128)S(1)} %fusion.5), kind=kCustom, calls=%fused_computation.9 | custom fusion | flops 262144 | bytes 3146240 | tf_op jit(solution)/shard_map/scatter-add | solution.py:17
  266.9 2.6 copy.102
  269.4 3.2 gather_fusion.4
  272.7 2.0 fusion.4
  274.8 0.1 slice.42
  274.9 0.6 slice.41
  275.4 0.1 convert_reduce_fusion.2
  275.5 0.6 fusion.23
  276.2 50.0 %reduce-scatter.6.cloned.1.call-done = f32[16,1024]{0,1:T(8,128)} async-done(((f32[16,8192]{0,1:T(8,128)}), f32[16,1024]{0,1:T(8,128)}) %reduce-scatter.6.cloned.1.call-update) | async-done | bytes 65552 | tf_op jit(solution)/shard_map/reduce_scatter | solution.py:93
  326.2 1.1 convert_element_type.38
  327.3 14.1 %all_gather.11 = bf16[16,8192]{0,1:T(8,128)(2,1)S(1)} all-gather(bf16[16,1024]{0,1:T(8,128)(2,1)S(1)} %convert_element_type.38), channel_id=1, replica_groups=mesh['row'=4,'col'=8] {'col'}, dimensions={1}, use_global_device_ids=true | all-gather | bytes 294912 | tf_op jit(solution)/shard_map/all_gather | solution.py:96
  341.4 0.8 copy.92
  342.2 0.6 gather_fusion.5
  342.8 0.4 fusion.11
  343.3 1.2 scatter_fusion.2
  344.5 0.1 copy.104
  344.6 0.9 gather_fusion.6
  345.4 0.1 bitcast_add_fusion.2
  345.6 0.6 copy-done.4
  346.2 0.7 copy.97
  347.0 18.9 %reduce-scatter.8.cloned.1.call-done = f32[16,256]{1,0:T(8,128)} async-done(((f32[16,1024]{1,0:T(8,128)}), f32[16,256]{1,0:T(8,128)}) %reduce-scatter.8.cloned.1.call-update) | async-done | bytes 16400 | tf_op jit(solution)/shard_map/reduce_scatter | solution.py:102
  365.8 1.3 convert_element_type.41
  (60 shorter events, 0.7 us)
Async XLA Ops:
  7.2 335.7 %copy-start = (bf16[16,128,128]{2,1,0:T(8,128)(2,1)S(1)}, bf16[16,128,128]{2,1,0:T(8,128)(2,1)}, u32[]{:S(2)}) copy-start(bf16[16,128,128]{2,1,0:T(8,128)(2,1)} %param.22) | copy-start | bytes 1572868
  7.2 22.7 %copy-start.8 = (s32[129]{0:T(256)S(1)}, s32[129]{0:T(256)}, u32[]{:S(2)}) copy-start(s32[129]{0:T(256)} %param.15) | copy-start | bytes 1552
  7.2 22.8 %copy-start.1 = (bf16[16,16384]{1,0:T(8,128)(2,1)S(1)}, bf16[16,16384]{1,0:T(8,128)(2,1)}, u32[]{:S(2)}) copy-start(bf16[16,16384]{1,0:T(8,128)(2,1)} %param.13) | copy-start | bytes 1572868
  7.2 22.6 %copy-start.5 = (s32[4096]{0:T(1024)S(1)}, s32[4096]{0:T(1024)}, u32[]{:S(2)}) copy-start(s32[4096]{0:T(1024)} %param.17) | copy-start | bytes 49156
  14.2 9.8 %all-to-all-start = ((s32[8,1,32]{2,1,0:T(1,128)}), s32[8,1,32]{2,1,0:T(1,128)S(1)}, u32[]{:S(2)}, u32[]{:S(2)}) async-start(s32[8,1,32]{2,1,0:T(1,128)} %all_to_all.13), calls=%async_computation | async-start | bytes 8192 | tf_op jit(solution)/shard_map/all_to_all | solution.py:75
  26.2 25.2 %all-to-all-start.1 = ((bf16[8,32,16,128]{3,2,1,0:T(8,128)(2,1)}), bf16[8,32,16,128]{3,2,1,0:T(8,128)(2,1)S(1)}, u32[]{:S(2)}, u32[]{:S(2)}) async-start(bf16[8,32,16,128]{3,2,1,0:T(8,128)(2,1)} %broadcast_select_fusion), calls=%async_computation.1 | async-start | bytes 2097152 | tf_op jit(solution)/shard_map/all_to_all | solution.py:77
  29.8 206.8 %reduce-scatter.4.cloned.1.call-start = ((), (), s32[]{:S(2)}) async-start(), calls=%async_computation.5 | async-start | bytes 10485760 | tf_op jit(solution)/shard_map/reduce_scatter | solution.py:83
  82.3 4.6 %copy-start.2 = (bf16[4096,16]{1,0:T(8,128)(2,1)S(1)}, bf16[4096,16]{1,0:T(8,128)(2,1)}, u32[]{:S(2)}) copy-start(bf16[4096,16]{1,0:T(8,128)(2,1)} %gather_fusion.2) | copy-start | bytes 393220
  89.9 0.7 copy-start.9
  89.9 1.3 copy-start.10
  89.9 1.3 copy-start.12
  89.9 2.1 copy-start.7
  89.9 2.1 copy-start.6
  90.0 236.3 %reduce-scatter.6.cloned.1.call-start = ((), (), s32[]{:S(2)}) async-start(), calls=%async_computation.6 | async-start | bytes 4718592 | tf_op jit(solution)/shard_map/reduce_scatter | solution.py:93
  238.6 22.6 %copy-start.3 = (bf16[16,4096]{1,0:T(8,128)(2,1)}, bf16[16,4096]{1,0:T(8,128)(2,1)S(1)}, u32[]{:S(2)}) copy-start(bf16[16,4096]{1,0:T(8,128)(2,1)S(1)} %copy.96) | copy-start | bytes 393220
  266.8 7.9 %copy-start.11 = (s32[9]{0:T(128)S(1)}, s32[9]{0:T(128)}, u32[]{:S(2)}) copy-start(s32[9]{0:T(128)} %param.23) | copy-start | bytes 112
  274.7 91.1 %reduce-scatter.8.cloned.1.call-start = ((), (), s32[]{:S(2)}) async-start(), calls=%async_computation.7 | async-start | bytes 81920 | tf_op jit(solution)/shard_map/reduce_scatter | solution.py:102
  345.6 0.6 copy-start.4
Sparse Core Ops, SparseCore 0:
  90.1 146.4 reduce-scatter.3
  274.8 51.3 reduce-scatter.5
  346.4 19.4 reduce-scatter.7
